TPU v7x, 32 devices: a whole 2x2x4 slice. The times are simulated.
32 devices in a mesh: cp: 8 (over z, x), tp: 4 (over y, core).
Axes of the slice: x: 2, y: 2, z: 4, core: 2. Of those that a mesh axis runs over, the one named last changes fastest.
Arguments:
- queries: bfloat16 [1536, 2048], P('cp', 'tp'), may hold values from -128 to 128
- keys: bfloat16 [1536, 256], P('cp'), may hold values from -6 to 6
- values: bfloat16 [1536, 256], P('cp'), may hold values from -6 to 6
- positions: int32 [1536], replicated, may hold values from 0 to 1535, as said below
- out_weight: bfloat16 [2048, 8192], P('tp'), may hold values from -0.125 to 0.125
Outputs:
- mixed: bfloat16 [1536, 8192], P(('cp', 'tp'))
Inputs may be any that keep to these rules, and one draw needn't show every extreme that they name: positions is a permutation of 0 to 1535. The tokens stored at indices d * 192 to (d + 1) * 192 - 1 form two runs of 96 consecutive positions, the first starting at b * 96 and the second at (15 - b) * 96 for some b, each b used by one d.
All inputs are finite; a program needn't handle non-finite values.
Results may differ from a plain program's by a relative error of at most 0.013.
Values may be sent and summed in bfloat16 or wider, within the bound.
A program may use at most 128 MiB of HBM per device.

v0:
```python
import jax
import jax.numpy as jnp
from jax import lax
from jax.sharding import PartitionSpec as P

HEAD = 128
GROUP = 8


def shards(queries, keys, values, positions, out_weight):
    tok_rows = queries.shape[0]
    head_count = queries.shape[1] // HEAD
    score_scale = HEAD ** (-0.5)
    kv_group = lax.axis_index("tp") * head_count // GROUP
    own_keys = lax.dynamic_slice_in_dim(keys, kv_group * HEAD, HEAD, 1)
    own_values = lax.dynamic_slice_in_dim(values, kv_group * HEAD, HEAD, 1)
    query_pos = lax.dynamic_slice_in_dim(positions, lax.axis_index("cp") * tok_rows, tok_rows, 0)
    local_queries = queries.reshape(tok_rows, head_count, HEAD)
    run_max = jnp.full((tok_rows, head_count), -1e30, jnp.float32)
    arrived_keys = lax.all_gather(own_keys, "cp", axis=0, tiled=True)
    arrived_values = lax.all_gather(own_values, "cp", axis=0, tiled=True)
    allowed = (positions[None, :] <= query_pos[:, None])[:, None, :]
    scores = (
        jnp.einsum("qhd,kd->qhk", local_queries, arrived_keys, preferred_element_type=jnp.float32)
        * score_scale
    )
    scores = jnp.where(allowed, scores, -1e30)
    new_max = jnp.maximum(run_max, jnp.max(scores, axis=-1))
    weights = jnp.where(allowed, jnp.exp(scores - new_max[:, :, None]), 0.0)
    run_sum = jnp.sum(weights, axis=-1)
    run_out = jnp.einsum(
        "qhk,kd->qhd",
        weights.astype(jnp.bfloat16),
        arrived_values,
        preferred_element_type=jnp.float32,
    )
    final_state = (new_max, run_sum, run_out)
    run_max, run_sum, run_out = final_state
    attended = (
        (run_out / run_sum[:, :, None]).astype(jnp.bfloat16).reshape(tok_rows, head_count * HEAD)
    )
    return lax.psum_scatter(
        jnp.dot(attended, out_weight, preferred_element_type=jnp.float32).astype(jnp.bfloat16),
        "tp",
        scatter_dimension=0,
        tiled=True,
    )


def solution(mesh):
    in_specs = (P("cp", "tp"), P("cp", None), P("cp", None), P(), P("tp", None))
    out_specs = P(("cp", "tp"), None)
    return jax.shard_map(shards, mesh=mesh, in_specs=in_specs, out_specs=out_specs, check_vma=False)
```

profile of v0, /device:TPU:0, one launch (start us, length us, event | category | flops | bytes accessed | tf_op | source)
XLA Modules:
  0.0 127.3 jit_solution(13655687156293303523)
XLA Ops:
  6.5 0.0 copy-start
  6.5 0.0 copy-start.1
  6.5 0.0 reduce-scatter.2.cloned.1.call-start
  6.5 0.8 constant_dynamic-slice_fusion.1
  7.4 32.8 %all_gather.6 = bf16[1536,128]{1,0:T(8,128)(2,1)S(1)} all-gather(bf16[192,128]{1,0:T(8,128)(2,1)S(1)} %constant_dynamic-slice_fusion.1), channel_id=1, replica_groups=mesh['cp'=8,'tp'=4] {'cp'}, dimensions={0}, use_global_device_ids=true | all-gather | bytes 442368 | tf_op jit(solution)/shard_map/all_gather | solution.py:20
  40.2 0.8 dynamic_slice.9
  40.9 0.9 broadcast_compare_fusion
  41.9 0.0 copy-done
  41.9 1.1 fusion
  43.0 0.0 copy-done.1
  43.0 31.0 %all_gather.7 = bf16[1536,128]{1,0:T(8,128)(2,1)S(1)} all-gather(bf16[192,128]{1,0:T(8,128)(2,1)S(1)} %constant_dynamic-slice_fusion), channel_id=1, replica_groups=mesh['cp'=8,'tp'=4] {'cp'}, dimensions={0}, use_global_device_ids=true | all-gather | bytes 442368 | tf_op jit(solution)/shard_map/all_gather | solution.py:21
  74.0 0.0 slice-start
  74.0 1.5 %fusion.1 = f32[192,4]{0,1:T(4,128)S(1)} fusion(f32[1536,192,4]{0,1,2:T(8,128)S(1)} %get-tuple-element.6, f32[192,4]{0,1:T(4,128)S(1)} %broadcast_maximum_fusion, pred[192,1536]{1,0:T(8,128)(4,1)S(1)} %broadcast_compare_fusion), kind=kLoop, calls=%fused_computation.4 | loop fusion | flops 5897472 | bytes 5019648 | tf_op jit(solution)/shard_map/reduce_sum | solution.py:30
  75.5 0.0 slice-start.1
  75.5 1.4 %fusion.12 = bf16[4,24,8,128]{3,2,1,0:T(8,128)(2,1)S(1)} fusion(f32[1536,192,4]{0,1,2:T(8,128)S(1)} %get-tuple-element.6, f32[192,4]{0,1:T(4,128)S(1)} %broadcast_maximum_fusion, pred[192,1536]{1,0:T(8,128)(4,1)S(1)} %broadcast_compare_fusion, bf16[1536,128]{1,0:T(8,128)(2,1)S(1)} %all_gather.7, f32[192,4]{0,1:T(4,128)S(1)} %fusion.1), kind=kOutput, calls=%fused_computation.10 | convolution fusion | flops 308084736 | bytes 5609472 | tf_op jit(solution)/shard_map/qhk,kd->qhd/dot_general | solution.py:31
  76.9 0.0 slice-done
  76.9 0.9 slice-done.1
  77.8 3.5 %convolution_convert_fusion = bf16[192,8192]{1,0:T(8,128)(2,1)} fusion(bf16[512,8192]{1,0:T(8,128)(2,1)S(1)} %bitcast.41, bf16[4,24,8,128]{3,2,1,0:T(8,128)(2,1)S(1)} %fusion.12), kind=kOutput, calls=%fused_computation | convolution fusion | flops 1612185600 | bytes 11730944 | tf_op jit(solution)/shard_map/dot_general | solution.py:43
  81.3 0.0 reduce-scatter.2.cloned.1.call-update
  81.3 39.2 %reduce-scatter.2.cloned.1.call-done = bf16[48,8192]{1,0:T(8,128)(2,1)} async-done(((bf16[192,8192]{1,0:T(8,128)(2,1)}), bf16[48,8192]{1,0:T(8,128)(2,1)}) %reduce-scatter.2.cloned.1.call-update) | async-done | bytes 786448 | tf_op jit(solution)/shard_map/reduce_scatter | solution.py:42
  (3 shorter events, 0.0 us)
Async XLA Ops:
  6.5 35.3 %copy-start = (bf16[192,512]{1,0:T(8,128)(2,1)S(1)}, bf16[192,512]{1,0:T(8,128)(2,1)}, u32[]{:S(2)}) copy-start(bf16[192,512]{1,0:T(8,128)(2,1)} %param.5) | copy-start | bytes 589828
  6.5 36.4 %copy-start.1 = (bf16[192,256]{1,0:T(8,128)(2,1)S(1)}, bf16[192,256]{1,0:T(8,128)(2,1)}, u32[]{:S(2)}) copy-start(bf16[192,256]{1,0:T(8,128)(2,1)} %param.7) | copy-start | bytes 294916
  6.5 114.0 %reduce-scatter.2.cloned.1.call-start = ((), (), s32[]{:S(2)}) async-start(), calls=%async_computation.1 | async-start | bytes 3932160 | tf_op jit(solution)/shard_map/reduce_scatter | solution.py:42
  74.0 2.9 %slice-start = ((s8[8388608]{0:T(1024)(128)(4,1)}), s8[4194304]{0:T(1024)(128)(4,1)S(1)}, s32[]{:S(2)}) async-start(s8[8388608]{0:T(1024)(128)(4,1)} %bitcast.40), calls=%async_computation.2 | async-start | bytes 8388608
  75.5 2.4 %slice-start.1 = ((s8[8388608]{0:T(1024)(128)(4,1)}), s8[4194304]{0:T(1024)(128)(4,1)S(1)}, s32[]{:S(2)}) async-start(s8[8388608]{0:T(1024)(128)(4,1)} %bitcast.40), calls=%async_computation.3 | async-start | bytes 8388608
Sparse Core Ops, SparseCore 0:
  81.4 39.0 reduce-scatter.1
where the time goes:
time: 128 us; the launch traced here: 127 us
  blocking collectives  63.7 us (50%)
  waiting for transfers between devices  39.2 us (31%)
  between operations  13.4 us (10%)
  matrix products  5.98 us (5%)
  local copies, waits for them, and re-layouts  2.58 us (2%)
  other arithmetic  2.41 us (2%)
    reduce_scatter x1, waiting for transfers between devices, shards(): lax.psum_scatter(jnp.dot(attended, out_weight, preferred_element_type=jnp...  39.2 us
    all_gather x1, blocking collectives, shards(): arrived_keys = lax.all_gather(own_keys, 'cp', axis=0, tiled=True)  32.8 us
    all_gather x1, blocking collectives, shards(): arrived_values = lax.all_gather(own_values, 'cp', axis=0, tiled=True)  31 us
    dot_general x1, matrix products, shards(): jnp.dot(attended, out_weight, preferred_element_type=jnp.float32)  3.47 us
  transfers between devices with their start and end apart: 1, of which 1 were waited for; matrix products, arithmetic and copies ran while one was open for 0% of the time, Pallas kernels for 0%

commit v1 on v0

--- a/solution.py
+++ b/solution.py
@@ -5,6 +5,12 @@
 
 HEAD = 128
 GROUP = 8
+
+
+def deliver_words_over_axis(page, which_dim):
+    arr_next = list(page.shape[1:])
+    arr_next[which_dim] *= page.shape[0]
+    return jnp.moveaxis(page, 0, which_dim).reshape(arr_next)
 
 
 def shards(queries, keys, values, positions, out_weight):
@@ -17,11 +23,36 @@
     query_pos = lax.dynamic_slice_in_dim(positions, lax.axis_index("cp") * tok_rows, tok_rows, 0)
     local_queries = queries.reshape(tok_rows, head_count, HEAD)
     run_max = jnp.full((tok_rows, head_count), -1e30, jnp.float32)
-    arrived_keys = lax.all_gather(own_keys, "cp", axis=0, tiled=True)
     arrived_values = lax.all_gather(own_values, "cp", axis=0, tiled=True)
     allowed = (positions[None, :] <= query_pos[:, None])[:, None, :]
+
+    def step_on_counts_all(xs, link_axis, on_dim, panel, d0):
+        carry_in = jax.lax.axis_index(link_axis)
+        block_last = jax.lax.axis_size(link_axis)
+        item_now, local_out, r1 = (block_last, carry_in, xs.shape[on_dim])
+        trail = []
+        before = xs
+        no = 0
+        slots = [(i, (i + 1) % item_now) for i in range(item_now)]
+        while no < item_now:
+            z1 = before if no == item_now - 1 else jax.lax.ppermute(before, link_axis, slots)
+            k_now = panel(before, (local_out - no) % item_now * r1)
+            trail.append(k_now)
+            before = z1
+            no = no + 1
+        trail = jnp.stack(trail, axis=0)[(local_out - jnp.arange(item_now)) % item_now]
+        return deliver_words_over_axis(trail, d0)
+
     scores = (
-        jnp.einsum("qhd,kd->qhk", local_queries, arrived_keys, preferred_element_type=jnp.float32)
+        step_on_counts_all(
+            own_keys,
+            "cp",
+            0,
+            lambda part, start: jnp.einsum(
+                "qhd,kd->qhk", local_queries, part, preferred_element_type=jnp.float32
+            ),
+            d0=2,
+        )
         * score_scale
     )
     scores = jnp.where(allowed, scores, -1e30)

time: 128 us -> 172 us (1.34)
  blocking collectives: 63.7 us -> 31.4 us
  waiting for transfers between devices: 39.2 us -> 69.4 us
  local copies, waits for them, and re-layouts: 2.58 us -> 24.3 us
  matrix products: 5.98 us -> 20.1 us
  other arithmetic: 2.41 us -> 10.3 us
  starting transfers between devices: 0.01 us -> 3.04 us
    ppermute x0 -> x7, waiting for transfers between devices: none -> 34 us  [step_on_counts_all(): jax.lax.ppermute(before, link_axis, slots)]
    all_gather x1 -> x0, blocking collectives: 32.8 us -> none  [shards(): arrived_keys = lax.all_gather(own_keys, 'cp', axis=0, tiled=True)]
    mul x0 -> x2, local copies, waits for them, and re-layouts: none -> 14.7 us  [shards(): step_on_counts_all(own_keys, 'cp', 0, lambda part, start: jnp.einsum('qhd...]
    dot_general x1 -> x8, matrix products: 1.11 us -> 9.51 us  [shards(): jnp.einsum('qhd,kd->qhk', local_queries, part, preferred_element_type=jnp...]
    mul x0 -> x1, other arithmetic: none -> 6.46 us  [shards(): step_on_counts_all(own_keys, 'cp', 0, lambda part, start: jnp.einsum('qhd...]
    gather x0 -> x1, local copies, waits for them, and re-layouts: none -> 6.37 us  [step_on_counts_all(): jnp.stack(trail, axis=0)[(local_out - jnp.arange(item_now)) % item_now]]
    reduce_scatter x1, waiting for transfers between devices: 39.2 us -> 35.4 us  [shards(): lax.psum_scatter(jnp.dot(attended, out_weight, preferred_element_type=jnp...]
    dot_general x1, matrix products: 3.47 us -> 6.94 us  [shards(): jnp.dot(attended, out_weight, preferred_element_type=jnp.float32)]
  transfers between devices with their start and end apart: 1 -> 8, of which waited for: 1 -> 7; matrix products, arithmetic and copies ran while one was open for 0% -> 7% of each run, Pallas kernels for 0% -> 0%
where the time goes in v1:
time: 172 us
  waiting for transfers between devices  69.4 us (40%)
  blocking collectives  31.4 us (18%)
  local copies, waits for them, and re-layouts  24.3 us (14%)
  matrix products  20.1 us (12%)
  between operations  13.4 us (8%)
  other arithmetic  10.3 us (6%)
  starting transfers between devices  3.04 us (2%)
    reduce_scatter x1, waiting for transfers between devices, shards(): lax.psum_scatter(jnp.dot(attended, out_weight, preferred_element_type=jnp...  35.4 us
    ppermute x7, waiting for transfers between devices, step_on_counts_all(): jax.lax.ppermute(before, link_axis, slots)  34 us
    all_gather x1, blocking collectives, shards(): arrived_values = lax.all_gather(own_values, 'cp', axis=0, tiled=True)  31.4 us
    mul x2, local copies, waits for them, and re-layouts, shards(): step_on_counts_all(own_keys, 'cp', 0, lambda part, start: jnp.einsum('qhd...  14.7 us
    dot_general x8, matrix products, shards(): jnp.einsum('qhd,kd->qhk', local_queries, part, preferred_element_type=jnp...  9.51 us
    dot_general x1, matrix products, shards(): jnp.dot(attended, out_weight, preferred_element_type=jnp.float32)  6.94 us
    mul x1, other arithmetic, shards(): step_on_counts_all(own_keys, 'cp', 0, lambda part, start: jnp.einsum('qhd...  6.46 us
    gather x1, local copies, waits for them, and re-layouts, step_on_counts_all(): jnp.stack(trail, axis=0)[(local_out - jnp.arange(item_now)) % item_now]  6.37 us
  transfers between devices with their start and end apart: 8, of which 7 were waited for; matrix products, arithmetic and copies ran while one was open for 7% of the time, Pallas kernels for 0%

profile of v1, /device:TPU:0, one launch (start us, length us, event | category | flops | bytes accessed | tf_op | source)
XLA Modules:
  0.0 171.9 jit_solution(16083450524662913446)
XLA Ops:
  6.5 0.0 copy-start
  6.5 0.0 reduce-scatter.2.cloned.1.call-start
  6.5 0.8 constant_dynamic-slice_fusion.1
  7.4 3.0 %collective-permute-start = (bf16[192,128]{1,0:T(8,128)(2,1)S(1)}, bf16[192,128]{1,0:T(8,128)(2,1)S(1)}, u32[]{:S(2)}, u32[]{:S(2)}) collective-permute-start(bf16[192,128]{1,0:T(8,128)(2,1)S(1)} %constant_dynamic-slice_fusion.1), channel_id=1, source_target_pairs={{0,4},{4,8},{8,12},{12,16},{16,20},{20,24},{24,28},{28,0},{1,5},{5... | collective-permute-start | bytes 147464 | tf_op jit(solution)/shard_map/ppermute | solution.py:38
  10.3 0.0 copy-done
  10.4 1.2 fusion.9
  11.5 0.8 le.29
  12.3 0.8 dynamic_slice.9
  13.1 0.9 broadcast_compare_fusion.1
  14.0 0.3 broadcast_compare_fusion
  14.3 0.8 constant_dynamic-slice_fusion
  15.1 31.4 %all_gather.3 = bf16[1536,128]{1,0:T(8,128)(2,1)S(1)} all-gather(bf16[192,128]{1,0:T(8,128)(2,1)S(1)} %constant_dynamic-slice_fusion), channel_id=1, replica_groups=mesh['cp'=8,'tp'=4] {'cp'}, dimensions={0}, use_global_device_ids=true | all-gather | bytes 442368 | tf_op jit(solution)/shard_map/all_gather | solution.py:26
  46.5 0.0 collective-permute-done
  46.5 0.1 collective-permute-start.1
  46.6 1.2 fusion.8
  47.7 5.6 %collective-permute-done.1 = bf16[192,128]{1,0:T(8,128)(2,1)S(1)} collective-permute-done((bf16[192,128]{1,0:T(8,128)(2,1)S(1)}, bf16[192,128]{1,0:T(8,128)(2,1)S(1)}, u32[]{:S(2)}, u32[]{:S(2)}) %collective-permute-start.1) | collective-permute-done | bytes 49184 | tf_op jit(solution)/shard_map/ppermute | solution.py:38
  53.3 0.0 collective-permute-start.2
  53.3 1.2 fusion.7
  54.6 5.5 %collective-permute-done.2 = bf16[192,128]{1,0:T(8,128)(2,1)S(1)} collective-permute-done((bf16[192,128]{1,0:T(8,128)(2,1)S(1)}, bf16[192,128]{1,0:T(8,128)(2,1)S(1)}, u32[]{:S(2)}, u32[]{:S(2)}) %collective-permute-start.2) | collective-permute-done | bytes 49184 | tf_op jit(solution)/shard_map/ppermute | solution.py:38
  60.1 0.0 collective-permute-start.3
  60.1 1.3 fusion.6
  61.4 5.5 %collective-permute-done.3 = bf16[192,128]{1,0:T(8,128)(2,1)S(1)} collective-permute-done((bf16[192,128]{1,0:T(8,128)(2,1)S(1)}, bf16[192,128]{1,0:T(8,128)(2,1)S(1)}, u32[]{:S(2)}, u32[]{:S(2)}) %collective-permute-start.3) | collective-permute-done | bytes 49184 | tf_op jit(solution)/shard_map/ppermute | solution.py:38
  66.9 0.0 collective-permute-start.4
  66.9 1.2 fusion.5
  68.1 6.1 %collective-permute-done.4 = bf16[192,128]{1,0:T(8,128)(2,1)S(1)} collective-permute-done((bf16[192,128]{1,0:T(8,128)(2,1)S(1)}, bf16[192,128]{1,0:T(8,128)(2,1)S(1)}, u32[]{:S(2)}, u32[]{:S(2)}) %collective-permute-start.4) | collective-permute-done | bytes 49184 | tf_op jit(solution)/shard_map/ppermute | solution.py:38
  74.2 0.0 collective-permute-start.5
  74.2 1.2 fusion.4
  75.4 5.6 %collective-permute-done.5 = bf16[192,128]{1,0:T(8,128)(2,1)S(1)} collective-permute-done((bf16[192,128]{1,0:T(8,128)(2,1)S(1)}, bf16[192,128]{1,0:T(8,128)(2,1)S(1)}, u32[]{:S(2)}, u32[]{:S(2)}) %collective-permute-start.5) | collective-permute-done | bytes 49184 | tf_op jit(solution)/shard_map/ppermute | solution.py:38
  81.0 0.0 collective-permute-start.6
  81.0 1.2 fusion.3
  82.1 5.6 %collective-permute-done.6 = bf16[192,128]{1,0:T(8,128)(2,1)S(1)} collective-permute-done((bf16[192,128]{1,0:T(8,128)(2,1)S(1)}, bf16[192,128]{1,0:T(8,128)(2,1)S(1)}, u32[]{:S(2)}, u32[]{:S(2)}) %collective-permute-start.6) | collective-permute-done | bytes 49184 | tf_op jit(solution)/shard_map/ppermute | solution.py:38
  87.8 1.2 fusion.2
  88.9 6.4 %gather_fusion = f32[8,192,4,192]{1,3,2,0:T(8,128)} fusion(f32[8,192,4,192]{1,3,2,0:T(8,128)} %fusion.2, s32[1024]{0:T(1024)S(1)} %pad_clamp_fusion), kind=kCustom, calls=%fused_computation | custom fusion | bytes 9437216 | tf_op jit(solution)/shard_map/gather | solution.py:43
  95.3 0.0 copy-start.1
  95.3 6.5 %multiply_bitcast_fusion = f32[192,4,8,192]{0,3,1,2:T(8,128)} fusion(f32[8,192,4,192]{1,3,2,0:T(8,128)} %gather_fusion), kind=kLoop, calls=%fused_computation.3 | loop fusion | flops 1179648 | bytes 9437184 | tf_op jit(solution)/shard_map/mul | solution.py:47
  101.8 0.0 copy-done.1
  101.8 0.9 select_reduce_fusion.1
  102.7 1.7 select_reduce_fusion
  104.4 7.2 %copy.22 = f32[192,4,8,192]{3,2,0,1:T(8,128)} copy(f32[192,4,8,192]{0,3,1,2:T(8,128)} %multiply_bitcast_fusion) | data formatting | bytes 9437184 | tf_op jit(solution)/shard_map/mul | solution.py:47
  111.6 7.5 %mul.31 = f32[192,4,1536]{2,0,1:T(8,128)} reshape(f32[192,4,8,192]{3,2,0,1:T(8,128)} %copy.22) | data formatting | bytes 9437184 | tf_op jit(solution)/shard_map/mul | solution.py:47
  119.1 3.6 %fusion.12 = bf16[4,24,8,128]{3,2,1,0:T(8,128)(2,1)S(1)} fusion(f32[192,4,1536]{2,0,1:T(8,128)} %mul.31, f32[192,4]{0,1:T(4,128)S(1)} %broadcast_maximum_fusion, pred[192,1536]{1,0:T(8,128)(4,1)S(1)} %broadcast_compare_fusion.1, bf16[1536,128]{1,0:T(8,128)(2,1)S(1)} %all_gather.3, f32[192,4]{0,1:T(4,128)S(1)} %select_reduce_fusion), kind=kOutput, calls=%fused_computation.26 | convolution fusion | flops 306905088 | bytes 5609472 | tf_op jit(solution)/shard_map/qhk,kd->qhd/dot_general | solution.py:62
  122.7 6.9 %convolution_convert_fusion = bf16[192,8192]{1,0:T(8,128)(2,1)} fusion(bf16[512,8192]{1,0:T(8,128)(2,1)} %param.9, bf16[4,24,8,128]{3,2,1,0:T(8,128)(2,1)S(1)} %fusion.12), kind=kOutput, calls=%fused_computation.1 | convolution fusion | flops 1612185600 | bytes 11730944 | tf_op jit(solution)/shard_map/dot_general | solution.py:74
  129.6 0.0 reduce-scatter.2.cloned.1.call-update
  129.6 35.4 %reduce-scatter.2.cloned.1.call-done = bf16[48,8192]{1,0:T(8,128)(2,1)} async-done(((bf16[192,8192]{1,0:T(8,128)(2,1)}), bf16[48,8192]{1,0:T(8,128)(2,1)}) %reduce-scatter.2.cloned.1.call-update) | async-done | bytes 786448 | tf_op jit(solution)/shard_map/reduce_scatter | solution.py:73
  (3 shorter events, 0.0 us)
Async XLA Ops:
  6.5 3.8 %copy-start = (bf16[192,512]{1,0:T(8,128)(2,1)S(1)}, bf16[192,512]{1,0:T(8,128)(2,1)}, u32[]{:S(2)}) copy-start(bf16[192,512]{1,0:T(8,128)(2,1)} %param.5) | copy-start | bytes 589828
  6.5 158.5 %reduce-scatter.2.cloned.1.call-start = ((), (), s32[]{:S(2)}) async-start(), calls=%async_computation.1 | async-start | bytes 3932160 | tf_op jit(solution)/shard_map/reduce_scatter | solution.py:73
  7.4 39.1 %collective-permute-start = (bf16[192,128]{1,0:T(8,128)(2,1)S(1)}, bf16[192,128]{1,0:T(8,128)(2,1)S(1)}, u32[]{:S(2)}, u32[]{:S(2)}) collective-permute-start(bf16[192,128]{1,0:T(8,128)(2,1)S(1)} %constant_dynamic-slice_fusion.1), channel_id=1, source_target_pairs={{0,4},{4,8},{8,12},{12,16},{16,20},{20,24},{24,28},{28,0},{1,5},{5... | collective-permute-start | bytes 147464 | tf_op jit(solution)/shard_map/ppermute | solution.py:38
  46.5 6.8 %collective-permute-start.1 = (bf16[192,128]{1,0:T(8,128)(2,1)S(1)}, bf16[192,128]{1,0:T(8,128)(2,1)S(1)}, u32[]{:S(2)}, u32[]{:S(2)}) collective-permute-start(bf16[192,128]{1,0:T(8,128)(2,1)S(1)} %collective-permute-done), channel_id=1, source_target_pairs={{0,4},{4,8},{8,12},{12,16},{16,20},{20,24},{24,28},{28,0},{1,5},{5... | collective-permute-start | bytes 147464 | tf_op jit(solution)/shard_map/ppermute | solution.py:38
  53.3 6.8 %collective-permute-start.2 = (bf16[192,128]{1,0:T(8,128)(2,1)S(1)}, bf16[192,128]{1,0:T(8,128)(2,1)S(1)}, u32[]{:S(2)}, u32[]{:S(2)}) collective-permute-start(bf16[192,128]{1,0:T(8,128)(2,1)S(1)} %collective-permute-done.1), channel_id=1, source_target_pairs={{0,4},{4,8},{8,12},{12,16},{16,20},{20,24},{24,28},{28,0},{1,5},{5... | collective-permute-start | bytes 147464 | tf_op jit(solution)/shard_map/ppermute | solution.py:38
  60.1 6.8 %collective-permute-start.3 = (bf16[192,128]{1,0:T(8,128)(2,1)S(1)}, bf16[192,128]{1,0:T(8,128)(2,1)S(1)}, u32[]{:S(2)}, u32[]{:S(2)}) collective-permute-start(bf16[192,128]{1,0:T(8,128)(2,1)S(1)} %collective-permute-done.2), channel_id=1, source_target_pairs={{0,4},{4,8},{8,12},{12,16},{16,20},{20,24},{24,28},{28,0},{1,5},{5... | collective-permute-start | bytes 147464 | tf_op jit(solution)/shard_map/ppermute | solution.py:38
  66.9 7.3 %collective-permute-start.4 = (bf16[192,128]{1,0:T(8,128)(2,1)S(1)}, bf16[192,128]{1,0:T(8,128)(2,1)S(1)}, u32[]{:S(2)}, u32[]{:S(2)}) collective-permute-start(bf16[192,128]{1,0:T(8,128)(2,1)S(1)} %collective-permute-done.3), channel_id=1, source_target_pairs={{0,4},{4,8},{8,12},{12,16},{16,20},{20,24},{24,28},{28,0},{1,5},{5... | collective-permute-start | bytes 147464 | tf_op jit(solution)/shard_map/ppermute | solution.py:38
  74.2 6.8 %collective-permute-start.5 = (bf16[192,128]{1,0:T(8,128)(2,1)S(1)}, bf16[192,128]{1,0:T(8,128)(2,1)S(1)}, u32[]{:S(2)}, u32[]{:S(2)}) collective-permute-start(bf16[192,128]{1,0:T(8,128)(2,1)S(1)} %collective-permute-done.4), channel_id=1, source_target_pairs={{0,4},{4,8},{8,12},{12,16},{16,20},{20,24},{24,28},{28,0},{1,5},{5... | collective-permute-start | bytes 147464 | tf_op jit(solution)/shard_map/ppermute | solution.py:38
  81.0 6.8 %collective-permute-start.6 = (bf16[192,128]{1,0:T(8,128)(2,1)S(1)}, bf16[192,128]{1,0:T(8,128)(2,1)S(1)}, u32[]{:S(2)}, u32[]{:S(2)}) collective-permute-start(bf16[192,128]{1,0:T(8,128)(2,1)S(1)} %collective-permute-done.5), channel_id=1, source_target_pairs={{0,4},{4,8},{8,12},{12,16},{16,20},{20,24},{24,28},{28,0},{1,5},{5... | collective-permute-start | bytes 147464 | tf_op jit(solution)/shard_map/ppermute | solution.py:38
  95.3 6.5 %copy-start.1 = (f32[8,192,4,192]{1,3,2,0:T(8,128)S(1)}, f32[8,192,4,192]{1,3,2,0:T(8,128)}, u32[]{:S(2)}) copy-start(f32[8,192,4,192]{1,3,2,0:T(8,128)} %gather_fusion) | copy-start | bytes 14155780
Sparse Core Ops, SparseCore 0:
  129.8 35.2 reduce-scatter.1
